TPU v7x, 32 devices: a whole 2x2x4 slice. The times are simulated.
32 devices in a mesh: tensor: 2 (over x), context: 8 (over z, core), dp: 2 (over y).
Axes of the slice: x: 2, y: 2, z: 4, core: 2. Of those that a mesh axis runs over, the one named last changes fastest.
Arguments:
- query_a: bfloat16 [2048, 1024], P(('dp', 'context'), 'tensor'), parts along dimension 0, may hold values from -5 to 5
- key_a: bfloat16 [2048, 256], P(('dp', 'context'), 'tensor'), parts along dimension 0, may hold values from -5 to 5
- value_a: bfloat16 [2048, 256], P(('dp', 'context'), 'tensor'), parts along dimension 0, may hold values from -12 to 12
- grad_out_a: bfloat16 [2048, 1024], P(('dp', 'context'), 'tensor'), parts along dimension 0, may hold values from -6 to 6
- query_b: bfloat16 [2048, 1024], P(('dp', 'context'), 'tensor'), parts along dimension 0, may hold values from -5 to 5
- key_b: bfloat16 [2048, 256], P(('dp', 'context'), 'tensor'), parts along dimension 0, may hold values from -5 to 5
- value_b: bfloat16 [2048, 256], P(('dp', 'context'), 'tensor'), parts along dimension 0, may hold values from -12 to 12
- slab_owner: int32 [8], replicated, may hold values from 0 to 7, each once
Outputs:
- out_b: bfloat16 [2048, 1024], P(('dp', 'context'), 'tensor'), parts along dimension 0
- grad_query_a: bfloat16 [2048, 1024], P(('dp', 'context'), 'tensor'), parts along dimension 0
- grad_key_a: bfloat16 [2048, 256], P(('dp', 'context'), 'tensor'), parts along dimension 0
- grad_value_a: bfloat16 [2048, 256], P(('dp', 'context'), 'tensor'), parts along dimension 0
There are 2 independent parts, one for each index of `dp`. A program takes and returns all parts, laid end to end along the dimension named above; an argument that names none is the same for every part. Nothing has to cross between parts.
Inputs may be any that keep to these rules, and one draw needn't show every extreme that they name: `slab_owner`: each number appears once.
All inputs are finite; a program needn't handle non-finite values.
Results may differ from a plain program's by a relative error of at most 0.0091.
Values may be sent and summed in bfloat16 or wider, within the bound.
No kernel may reach another device: no remote copies, remote signals or barrier semaphores. Data moves between devices by JAX's collectives and lax.ppermute only.
A program may use at most 64 MiB of HBM per device.

v0:
```python
from functools import partial
import math

import jax
import jax.numpy as jnp
from jax import lax
from jax.experimental import pallas as pl
from jax.experimental.pallas import tpu as pltpu
from jax.sharding import PartitionSpec as P


LOW = -1e30
FLOOR = -1e20
F32 = jnp.float32
BF16 = jnp.bfloat16
LOG2E = math.log2(math.e)
VMEM_GRANT = 24 << 20


def dot(a, b, dims):
    return lax.dot_general(a, b, (dims, ((), ())), preferred_element_type=F32)


class Shape:
    def __init__(self, tok, width, dim, devices):
        self.tok, self.width, self.dim, self.devices = tok, width, dim, devices
        self.half = tok // 2
        self.heads = width // dim
        self.chunks = devices // 2
        self.group = self.heads * self.half
        self.keys = self.chunks * self.half
        self.scale = dim ** (-0.5)
        self.exp_scale = self.scale * LOG2E


def stacked(s, own_ref, other_ref):
    parts = []
    for h in range(2):
        for ref in (own_ref, other_ref):
            for g in range(s.heads):
                parts.append(ref[h * s.half:(h + 1) * s.half, g * s.dim:(g + 1) * s.dim])
    return jnp.concatenate(parts, axis=0)


def halves(s, chunk_refs, part):
    cols = slice(part * s.dim, (part + 1) * s.dim)
    low = jnp.concatenate([r[:s.half, cols] for r in chunk_refs], axis=0)
    high = jnp.concatenate([r[s.half:, cols] for r in chunk_refs], axis=0)
    return low, high


def relative(s):
    key = lax.broadcasted_iota(jnp.int32, (s.half, s.group), 0)
    row = lax.broadcasted_iota(jnp.int32, (s.half, s.group), 1) % s.half
    return key - row


def masked(s, scores, rel, gap_ref, d, high):
    parts = []
    for k in range(s.chunks):
        gap = gap_ref[d * s.chunks + k:d * s.chunks + k + 1, :]
        block = scores[k * s.half:(k + 1) * s.half, :]
        parts.append(jnp.where(rel <= (-gap if high else gap), block, LOW))
    return jnp.concatenate(parts, axis=0)


def fetch_kernel(s, owner, ka, va, qa, ga, kb, vb, qb, kv_a, kv_b, query_a, grad_a, query_b, gap, slabs, sems):
    cols = [pl.ds(i * s.dim, s.dim) for i in range(2)]
    moves = [
        (owner, slabs), (ka, kv_a.at[:, cols[0]]), (va, kv_a.at[:, cols[1]]),
        (kb, kv_b.at[:, cols[0]]), (vb, kv_b.at[:, cols[1]]),
        (qa, query_a), (ga, grad_a), (qb, query_b),
    ]
    copies = [pltpu.make_async_copy(a, b, sems.at[i]) for i, (a, b) in enumerate(moves)]
    for c in copies:
        c.start()
    copies[0].wait()
    me = lax.axis_index("context")
    for d in range(2):
        for k in range(s.chunks):
            ahead = (slabs[me ^ d] - slabs[me ^ (2 * k)]) * s.half
            gap[d * s.chunks + k:d * s.chunks + k + 1, :] = jnp.full((1, s.group), ahead, jnp.int32)
    for c in copies[1:]:
        c.wait()


def stack_kernel(s, *refs):
    count = len(refs) // 3
    for i in range(count):
        refs[2 * count + i][...] = stacked(s, refs[2 * i], refs[2 * i + 1])


def pack_kernel(*refs):
    at = 0
    for ref in refs[:-1]:
        refs[-1][at:at + ref.shape[0]] = ref[...]
        at += ref.shape[0]


def stats_kernel(s, gap_ref, q_ref, g_ref, *refs):
    chunks, out_ref = refs[:-1], refs[-1]
    q, g = q_ref[...], g_ref[...]
    k_low, k_high = halves(s, chunks, 0)
    v_low, v_high = halves(s, chunks, 1)
    rel = relative(s)
    for h in range(2):
        for d in range(2):
            at = (2 * h + d) * s.group
            qt, gt = q[at:at + s.group], g[at:at + s.group]
            raw = dot(k_low, qt, ((1,), (1,)))
            pg = dot(v_low, gt, ((1,), (1,)))
            if h == 0:
                raw = masked(s, raw, rel, gap_ref, d, False)
                blocks = [(raw, pg)]
            else:
                more = masked(s, dot(k_high, qt, ((1,), (1,))), rel, gap_ref, d, True)
                blocks = [(raw, pg), (more, dot(v_high, gt, ((1,), (1,))))]
            top = jnp.full((1, s.group), FLOOR, F32)
            for raw, pg in blocks:
                top = jnp.maximum(top, jnp.max(raw, axis=0, keepdims=True))
            total = jnp.zeros((1, s.group), F32)
            dsum = jnp.zeros((1, s.group), F32)
            for raw, pg in blocks:
                p = jnp.exp2((raw - top) * s.exp_scale)
                total = total + jnp.sum(p, axis=0, keepdims=True)
                dsum = dsum + jnp.sum(p * pg, axis=0, keepdims=True)
            out_ref[0:1, at:at + s.group] = top
            out_ref[1:2, at:at + s.group] = total
            out_ref[2:3, at:at + s.group] = dsum
    out_ref[3:8, :] = jnp.zeros((5, 4 * s.group), F32)


def back_kernel(s, gap_ref, q_ref, g_ref, mine_ref, theirs_ref, *refs):
    chunks = refs[:s.chunks]
    outs = refs[s.chunks:2 * s.chunks]
    dq_own_ref, dq_other_ref, prob_ref, grad_ref = refs[2 * s.chunks:]
    q, g = q_ref[...], g_ref[...]
    k_low, k_high = halves(s, chunks, 0)
    v_low, v_high = halves(s, chunks, 1)
    rel = relative(s)
    group, keys = s.group, s.keys
    for h in range(2):
        for d in range(2):
            at, across = (2 * h + d) * group, (2 * h + 1 - d) * group
            m1, l1, d1 = (mine_ref[i:i + 1, at:at + group] for i in range(3))
            m2, l2, d2 = (theirs_ref[i:i + 1, across:across + group] for i in range(3))
            top = jnp.maximum(m1, m2)
            w1, w2 = jnp.exp2((m1 - top) * s.exp_scale), jnp.exp2((m2 - top) * s.exp_scale)
            total = l1 * w1 + l2 * w2
            delta = (d1 * w1 + d2 * w2) / total
            shift = top * s.exp_scale + jnp.log2(total)
            qt, gt = q[at:at + group], g[at:at + group]
            for b in range(h + 1):
                kk, vv = (k_low, v_low) if b == 0 else (k_high, v_high)
                raw = dot(kk, qt, ((1,), (1,)))
                pg = dot(vv, gt, ((1,), (1,)))
                if b == h:
                    raw = masked(s, raw, rel, gap_ref, d, h == 1)
                p = jnp.exp2(raw * s.exp_scale - shift)
                prob_ref[b * keys:(b + 1) * keys, at:at + group] = p.astype(BF16)
                grad_ref[b * keys:(b + 1) * keys, at:at + group] = (p * (pg - delta)).astype(BF16)
    mid = 2 * group
    dk_low = dot(grad_ref[:keys, :], q, ((1,), (0,))) * s.scale
    dv_low = dot(prob_ref[:keys, :], g, ((1,), (0,)))
    dk_high = dot(grad_ref[keys:, mid:], q[mid:], ((1,), (0,))) * s.scale
    dv_high = dot(prob_ref[keys:, mid:], g[mid:], ((1,), (0,)))
    for k in range(s.chunks):
        at = slice(k * s.half, (k + 1) * s.half)
        kind = outs[k].dtype
        outs[k][:s.half, :s.dim] = dk_low[at].astype(kind)
        outs[k][:s.half, s.dim:] = dv_low[at].astype(kind)
        outs[k][s.half:, :s.dim] = dk_high[at].astype(kind)
        outs[k][s.half:, s.dim:] = dv_high[at].astype(kind)
    low_rows = dot(k_low, grad_ref[:keys, :mid], ((0,), (0,)))
    high_rows = dot(k_low, grad_ref[:keys, mid:], ((0,), (0,)))
    high_rows = high_rows + dot(k_high, grad_ref[keys:, mid:], ((0,), (0,)))
    for d, ref in enumerate((dq_own_ref, dq_other_ref)):
        ref[:, :group] = low_rows[:, d * group:(d + 1) * group]
        ref[:, group:] = high_rows[:, d * group:(d + 1) * group]


def forward_kernel(s, names, gap_ref, q_ref, *refs):
    chunks, outs = refs[:-2], refs[-2:]
    q = q_ref[...]
    blocks = [r[k * s.tok:(k + 1) * s.tok] for r in chunks for k in range(r.shape[0] // s.tok)]
    blocks = [blocks[names.index(k)] for k in range(s.chunks)]
    k_low, k_high = halves(s, blocks, 0)
    v_low, v_high = halves(s, blocks, 1)
    rel = relative(s)
    for h in range(2):
        for d in range(2):
            at = (2 * h + d) * s.group
            qt = q[at:at + s.group]
            raw = dot(k_low, qt, ((1,), (1,)))
            if h == 0:
                blocks = [(masked(s, raw, rel, gap_ref, d, False), v_low)]
            else:
                more = dot(k_high, qt, ((1,), (1,)))
                more = masked(s, more, rel, gap_ref, d, True)
                blocks = [(raw, v_low), (more, v_high)]
            top = jnp.full((1, s.group), FLOOR, F32)
            for raw, vv in blocks:
                top = jnp.maximum(top, jnp.max(raw, axis=0, keepdims=True))
            total = jnp.zeros((1, s.group), F32)
            acc = jnp.zeros((s.dim, s.group), F32)
            for raw, vv in blocks:
                p = jnp.exp2((raw - top) * s.exp_scale)
                total = total + jnp.sum(p, axis=0, keepdims=True)
                acc = acc + dot(vv, p.astype(BF16), ((0,), (0,)))
            cols = slice(h * s.group, (h + 1) * s.group)
            outs[d][:s.dim, cols] = acc
            outs[d][s.dim:s.dim + 1, cols] = top
            outs[d][s.dim + 1:s.dim + 2, cols] = total
            outs[d][s.dim + 2:s.dim + 8, cols] = jnp.zeros((6, s.group), F32)


def rows_from(s, wide, out_ref):
    for h in range(2):
        for g in range(s.heads):
            at = h * s.group + g * s.half
            block = wide[:, at:at + s.half]
            out_ref[h * s.half:(h + 1) * s.half, g * s.dim:(g + 1) * s.dim] = block.T.astype(BF16)


def query_kernel(s, own_ref, other_ref, out_ref):
    rows_from(s, (own_ref[...] + other_ref[...]) * s.scale, out_ref)


def merge_kernel(s, own_ref, other_ref, out_ref):
    d = s.dim
    m1, l1 = own_ref[d:d + 1, :], own_ref[d + 1:d + 2, :]
    m2, l2 = other_ref[d:d + 1, :], other_ref[d + 1:d + 2, :]
    top = jnp.maximum(m1, m2)
    w1, w2 = jnp.exp2((m1 - top) * s.exp_scale), jnp.exp2((m2 - top) * s.exp_scale)
    total = l1 * w1 + l2 * w2
    rows_from(s, own_ref[:d, :] * (w1 / total) + other_ref[:d, :] * (w2 / total), out_ref)


def sum_kernel(s, *refs):
    terms, (key_ref, value_ref) = refs[:-2], refs[-2:]
    acc = terms[0][...]
    for t in terms[1:]:
        acc = acc + t[...].astype(F32)
    key_ref[...] = acc[:, :s.dim].astype(BF16)
    value_ref[...] = acc[:, s.dim:].astype(BF16)


def call(kernel, outs, args, flops, scratch=(), space=pltpu.VMEM):
    specs = [pl.BlockSpec(memory_space=space)] * len(args)
    if space == pltpu.HBM:
        args = [pltpu.with_memory_space_constraint(a, space) for a in args]
    return pl.pallas_call(
        kernel,
        out_shape=outs,
        in_specs=specs,
        out_specs=jax.tree.map(lambda _: pl.BlockSpec(memory_space=pltpu.VMEM), outs),
        scratch_shapes=scratch,
        compiler_params=pltpu.CompilerParams(vmem_limit_bytes=VMEM_GRANT),
        cost_estimate=pl.CostEstimate(flops=flops, bytes_accessed=1 << 20, transcendentals=0),
    )(*args)


def on_device(query_a, key_a, value_a, grad_out_a, query_b, key_b, value_b, slab_owner):
    devices = lax.axis_size("context")
    tok, width = query_a.shape
    s = Shape(tok, width, key_a.shape[1], devices)
    dim, group = s.dim, s.group

    def swapped(x, bits):
        return lax.ppermute(x, "context", [(i, i ^ bits) for i in range(devices)])

    def sds(shape, dtype):
        return jax.ShapeDtypeStruct(shape, dtype)

    unit = 2 * 4 * group * s.keys * dim
    wide, pair, stack = sds((tok, width), BF16), sds((tok, 2 * dim), BF16), sds((4 * group, dim), BF16)
    kv_a, kv_b, query_a, grad_a, query_b, gap = call(
        partial(fetch_kernel, s), [pair, pair, wide, wide, wide, sds((2 * s.chunks, group), jnp.int32)],
        [slab_owner, key_a, value_a, query_a, grad_out_a, key_b, value_b, query_b], unit,
        space=pltpu.HBM, scratch=[pltpu.SMEM((devices,), jnp.int32), pltpu.SemaphoreType.DMA((8,))],
    )
    held, bit = {0: kv_a}, s.chunks // 2
    while bit:
        held.update({k ^ bit: swapped(x, 2 * bit) for k, x in list(held.items())})
        bit //= 2
    kv_a = [held[k] for k in range(s.chunks)]
    query_p, grad_p = swapped(query_a, 1), swapped(grad_a, 1)
    query_bp = swapped(query_b, 1)
    q_a, g_a = call(partial(stack_kernel, s), [stack, stack], [query_a, query_p, grad_a, grad_p], unit)
    mine = call(partial(stats_kernel, s), sds((8, 4 * group), F32), [gap, q_a, g_a, *kv_a], 8 * unit)
    order_b, bit = [0], s.chunks // 2
    while bit:
        if len(order_b) > 1:
            kv_b = call(pack_kernel, sds((len(order_b) * tok, 2 * dim), BF16), parts, unit)
        parts = [kv_b, swapped(kv_b, 2 * bit)]
        order_b += [k ^ bit for k in order_b]
        bit //= 2
    kv_b = parts
    theirs = swapped(mine, 1)
    kinds = [F32] + [BF16] * (s.chunks - 1)
    back = call(
        partial(back_kernel, s),
        [sds((tok, 2 * dim), kind) for kind in kinds] + [sds((dim, 2 * group), F32)] * 2,
        [gap, q_a, g_a, mine, theirs, *kv_a], 20 * unit,
        scratch=[pltpu.VMEM((2 * s.keys, 4 * group), BF16)] * 2,
    )
    terms, (dq_own, dq_other) = back[:s.chunks], back[s.chunks:]
    terms = [terms[0]] + [swapped(terms[k], 2 * k) for k in range(1, s.chunks)]
    dq_got = swapped(dq_other, 1)

    (q_b,) = call(partial(stack_kernel, s), [stack], [query_b, query_bp], unit)
    part_own, part_other = call(
        partial(forward_kernel, s, order_b), [sds((dim + 8, 2 * group), F32)] * 2,
        [gap, q_b, *kv_b], 10 * unit,
    )
    part_got = swapped(part_other, 1)
    grad_query_a = call(partial(query_kernel, s), sds((tok, width), BF16), [dq_own, dq_got], unit)
    out_b = call(partial(merge_kernel, s), sds((tok, width), BF16), [part_own, part_got], unit)
    grad_key_a, grad_value_a = call(partial(sum_kernel, s), [sds((tok, dim), BF16)] * 2, terms, unit)
    return (out_b, grad_query_a, grad_key_a, grad_value_a)


def solution(mesh):
    rows = P(("dp", "context"), "tensor")

    return jax.shard_map(
        on_device,
        mesh=mesh,
        in_specs=(rows,) * 7 + (P(),),
        out_specs=(rows,) * 4,
        check_vma=False,
    )
```

profile of v0, /device:TPU:0, one launch (start us, length us, event | category | flops | bytes accessed | tf_op | source)
XLA Modules:
  0.0 36.7 jit_solution(9605690563262022071)
XLA Ops:
  0.6 1.2 %shard_map.111 = (bf16[128,256]{1,0:T(8,128)(2,1)S(1)}, bf16[128,256]{1,0:T(8,128)(2,1)S(1)}, bf16[128,512]{1,0:T(8,128)(2,1)S(1)}, bf16[128,512]{1,0:T(8,128)(2...) custom-call(s32[8]{0:T(128)} %owner.1, bf16[128,128]{1,0:T(8,128)(2,1)} %ka.1, bf16[128,128]{1,0:T(8,128)(2,1)} %va.1, ...), custom_call_target="tpu_custom_call" | custom-call | flops 67108864 | bytes 1048576 | tf_op jit(solution)/shard_map/pallas_call | solution.py:252
  1.8 0.6 %collective-permute-start.4 = (bf16[128,512]{1,0:T(8,128)(2,1)S(1)}, bf16[128,512]{1,0:T(8,128)(2,1)S(1)}, u32[]{:S(2)}, u32[]{:S(2)}) collective-permute-start(bf16[128,512]{1,0:T(8,128)(2,1)S(1)} %get-tuple-element.27.refs_0_), channel_id=1, source_target_pairs={{0,2},{2,0},{4,6},{6,4},{8,10},{10,8},{12,14},{14,12},{1,3},{3,1},... | collective-permute-start | bytes 393224 | tf_op jit(solution)/shard_map/ppermute | solution.py:270
  2.4 3.7 %collective-permute-start.1 = (bf16[128,256]{1,0:T(8,128)(2,1)S(1)}, bf16[128,256]{1,0:T(8,128)(2,1)S(1)}, u32[]{:S(2)}, u32[]{:S(2)}) collective-permute-start(bf16[128,256]{1,0:T(8,128)(2,1)S(1)} %get-tuple-element.24.refs_0_), channel_id=1, source_target_pairs={{0,8},{2,10},{4,12},{6,14},{8,0},{10,2},{12,4},{14,6},{1,9},{3,11}... | collective-permute-start | bytes 196616 | tf_op jit(solution)/shard_map/ppermute | solution.py:270
  6.0 0.2 collective-permute-start.5
  6.2 0.3 collective-permute-start.7
  6.5 0.1 collective-permute-start
  6.5 3.7 %collective-permute-done.1.refs_1_ = bf16[128,256]{1,0:T(8,128)(2,1)S(1)} collective-permute-done((bf16[128,256]{1,0:T(8,128)(2,1)S(1)}, bf16[128,256]{1,0:T(8,128)(2,1)S(1)}, u32[]{:S(2)}, u32[]{:S(2)}) %collective-permute-start.1) | collective-permute-done | bytes 65568 | tf_op jit(solution)/shard_map/ppermute | solution.py:270
  10.2 2.2 %collective-permute-start.2 = (bf16[256,256]{1,0:T(8,128)(2,1)S(1)}, bf16[256,256]{1,0:T(8,128)(2,1)S(1)}, u32[]{:S(2)}, u32[]{:S(2)}) collective-permute-start(bf16[256,256]{1,0:T(8,128)(2,1)S(1)} %shard_map.113.refs_0_), channel_id=1, source_target_pairs={{0,4},{2,6},{4,0},{6,2},{8,12},{10,14},{12,8},{14,10},{1,5},{3,7},... | collective-permute-start | bytes 393224 | tf_op jit(solution)/shard_map/ppermute | solution.py:270
  12.4 0.6 %collective-permute-done.7.refs_2_ = bf16[128,256]{1,0:T(8,128)(2,1)S(1)} collective-permute-done((bf16[128,256]{1,0:T(8,128)(2,1)S(1)}, bf16[128,256]{1,0:T(8,128)(2,1)S(1)}, u32[]{:S(2)}, u32[]{:S(2)}) %collective-permute-start.7) | collective-permute-done | bytes 65568 | tf_op jit(solution)/shard_map/ppermute | solution.py:270
  12.9 0.7 %collective-permute-start.6 = (bf16[128,256]{1,0:T(8,128)(2,1)S(1)}, bf16[128,256]{1,0:T(8,128)(2,1)S(1)}, u32[]{:S(2)}, u32[]{:S(2)}) collective-permute-start(bf16[128,256]{1,0:T(8,128)(2,1)S(1)} %get-tuple-element.31.refs_0_), channel_id=1, source_target_pairs={{0,4},{2,6},{4,0},{6,2},{8,12},{10,14},{12,8},{14,10},{1,5},{3,7},... | collective-permute-start | bytes 196616 | tf_op jit(solution)/shard_map/ppermute | solution.py:270
  13.7 0.0 collective-permute-done.4.refs_1_
  13.7 1.3 %collective-permute-start.8 = (bf16[128,256]{1,0:T(8,128)(2,1)S(1)}, bf16[128,256]{1,0:T(8,128)(2,1)S(1)}, u32[]{:S(2)}, u32[]{:S(2)}) collective-permute-start(bf16[128,256]{1,0:T(8,128)(2,1)S(1)} %collective-permute-done.7.refs_2_), channel_id=1, source_target_pairs={{0,4},{2,6},{4,0},{6,2},{8,12},{10,14},{12,8},{14,10},{1,5},{3,7},... | collective-permute-start | bytes 196616 | tf_op jit(solution)/shard_map/ppermute | solution.py:270
  15.0 0.0 collective-permute-done.5.refs_3_
  15.0 0.1 shard_map.116
  15.1 3.1 %collective-permute-done.6.refs_1_ = bf16[128,256]{1,0:T(8,128)(2,1)S(1)} collective-permute-done((bf16[128,256]{1,0:T(8,128)(2,1)S(1)}, bf16[128,256]{1,0:T(8,128)(2,1)S(1)}, u32[]{:S(2)}, u32[]{:S(2)}) %collective-permute-start.6) | collective-permute-done | bytes 65568 | tf_op jit(solution)/shard_map/ppermute | solution.py:270
  18.1 0.7 %collective-permute-done.8.refs_3_ = bf16[128,256]{1,0:T(8,128)(2,1)S(1)} collective-permute-done((bf16[128,256]{1,0:T(8,128)(2,1)S(1)}, bf16[128,256]{1,0:T(8,128)(2,1)S(1)}, u32[]{:S(2)}, u32[]{:S(2)}) %collective-permute-start.8) | collective-permute-done | bytes 65568 | tf_op jit(solution)/shard_map/ppermute | solution.py:270
  18.9 0.8 %shard_map.117.mine_ref = f32[8,1024]{1,0:T(8,128)S(1)} custom-call(s32[8,256]{1,0:T(8,128)S(1)} %get-tuple-element.22.gap_ref, bf16[1024,128]{1,0:T(8,128)(2,1)S(1)} %get-tuple-element.29.q_ref, bf16[1024,128]{1,0:T(8,128)(2,1)S(1)} %get-tuple-element.30.g_ref, bf16[128,256]{1,0:T(8,128)(2,1)S(1)} %get-tuple-element.31.refs_0_, ...), custom_call_target="tpu_custom_call" | custom-call | flops 536870912 | bytes 1048576 | tf_op jit(solution)/shard_map/pallas_call | solution.py:252
  19.7 0.1 collective-permute-start.9
  19.7 0.0 collective-permute-done.refs_1_
  19.8 0.0 collective-permute-done.2.refs_1_
  19.8 1.5 %shard_map.114 = (f32[136,512]{1,0:T(8,128)S(1)}, f32[136,512]{1,0:T(8,128)S(1)}) custom-call(s32[8,256]{1,0:T(8,128)S(1)} %get-tuple-element.22.gap_ref, bf16[1024,128]{1,0:T(8,128)(2,1)S(1)} %shard_map.112.q_ref, bf16[256,256]{1,0:T(8,128)(2,1)S(1)} %shard_map.113.refs_0_, bf16[256,256]{1,0:T(8,128)(2,1)S(1)} %collective-permute-done.2.refs_1_), custom_call_target="tpu_custom_call" | custom-call | flops 671088640 | bytes 1048576 | tf_op jit(solution)/shard_map/pallas_call | solution.py:252
  21.3 0.5 %collective-permute-start.3 = (f32[136,512]{1,0:T(8,128)S(1)}, f32[136,512]{1,0:T(8,128)S(1)}, u32[]{:S(2)}, u32[]{:S(2)}) collective-permute-start(f32[136,512]{1,0:T(8,128)S(1)} %get-tuple-element.26), channel_id=1, source_target_pairs={{0,2},{2,0},{4,6},{6,4},{8,10},{10,8},{12,14},{14,12},{1,3},{3,1},... | collective-permute-start | bytes 835592 | tf_op jit(solution)/shard_map/ppermute | solution.py:270
  21.8 0.0 collective-permute-done.9.theirs_ref
  21.8 1.1 %shard_map.118 = (f32[128,256]{1,0:T(8,128)S(1)}, bf16[128,256]{1,0:T(8,128)(2,1)S(1)}, bf16[128,256]{1,0:T(8,128)(2,1)S(1)}, bf16[128,256]{1,0:T(8,128)(2,1)S(1...) custom-call(s32[8,256]{1,0:T(8,128)S(1)} %get-tuple-element.22.gap_ref, ...), custom_call_target="tpu_custom_call" | custom-call | flops 1342177280 | bytes 1048576 | tf_op jit(solution)/shard_map/pallas_call | solution.py:252
  22.9 0.1 collective-permute-start.10
  23.0 1.8 %collective-permute-start.11 = (bf16[128,256]{1,0:T(8,128)(2,1)S(1)}, bf16[128,256]{1,0:T(8,128)(2,1)S(1)}, u32[]{:S(2)}, u32[]{:S(2)}) collective-permute-start(bf16[128,256]{1,0:T(8,128)(2,1)S(1)} %get-tuple-element.35), channel_id=1, source_target_pairs={{0,4},{2,6},{4,0},{6,2},{8,12},{10,14},{12,8},{14,10},{1,5},{3,7},... | collective-permute-start | bytes 196616 | tf_op jit(solution)/shard_map/ppermute | solution.py:270
  24.8 3.4 %collective-permute-start.12 = (bf16[128,256]{1,0:T(8,128)(2,1)S(1)}, bf16[128,256]{1,0:T(8,128)(2,1)S(1)}, u32[]{:S(2)}, u32[]{:S(2)}) collective-permute-start(bf16[128,256]{1,0:T(8,128)(2,1)S(1)} %get-tuple-element.36), channel_id=1, source_target_pairs={{0,8},{2,10},{4,12},{6,14},{8,0},{10,2},{12,4},{14,6},{1,9},{3,11}... | collective-permute-start | bytes 196616 | tf_op jit(solution)/shard_map/ppermute | solution.py:270
  28.2 0.0 collective-permute-start.13
  28.2 0.0 collective-permute-done.11.refs_1_
  28.2 4.3 %collective-permute-done.12.refs_2_ = bf16[128,256]{1,0:T(8,128)(2,1)S(1)} collective-permute-done((bf16[128,256]{1,0:T(8,128)(2,1)S(1)}, bf16[128,256]{1,0:T(8,128)(2,1)S(1)}, u32[]{:S(2)}, u32[]{:S(2)}) %collective-permute-start.12) | collective-permute-done | bytes 65568 | tf_op jit(solution)/shard_map/ppermute | solution.py:270
  32.5 1.7 %collective-permute-done.13.refs_3_ = bf16[128,256]{1,0:T(8,128)(2,1)S(1)} collective-permute-done((bf16[128,256]{1,0:T(8,128)(2,1)S(1)}, bf16[128,256]{1,0:T(8,128)(2,1)S(1)}, u32[]{:S(2)}, u32[]{:S(2)}) %collective-permute-start.13) | collective-permute-done | bytes 65568 | tf_op jit(solution)/shard_map/ppermute | solution.py:270
  34.3 0.7 %shard_map.120 = (bf16[128,128]{1,0:T(8,128)(2,1)}, bf16[128,128]{1,0:T(8,128)(2,1)}) custom-call(f32[128,256]{1,0:T(8,128)S(1)} %get-tuple-element.34.refs_0_, bf16[128,256]{1,0:T(8,128)(2,1)S(1)} %collective-permute-done.11.refs_1_, bf16[128,256]{1,0:T(8,128)(2,1)S(1)} %collective-permute-done.12.refs_2_, bf16[128,256]{1,0:T(8,128)(2,1)S(1)} %collective-permute-done.13.refs_3_), custom_call_target="tpu_custom_call" | custom-call | flops 67108864 | bytes 1048576 | tf_op jit(solution)/shard_map/pallas_call | solution.py:252
  34.9 0.0 collective-permute-done.10.other_ref
  34.9 0.9 %shard_map.119 = bf16[128,512]{1,0:T(8,128)(2,1)} custom-call(f32[128,512]{1,0:T(8,128)S(1)} %get-tuple-element.32.own_ref, f32[128,512]{1,0:T(8,128)S(1)} %collective-permute-done.10.other_ref), custom_call_target="tpu_custom_call" | custom-call | flops 67108864 | bytes 1048576 | tf_op jit(solution)/shard_map/pallas_call | solution.py:252
  35.8 0.0 collective-permute-done.3.other_ref
  35.8 0.9 %shard_map.115 = bf16[128,512]{1,0:T(8,128)(2,1)} custom-call(f32[136,512]{1,0:T(8,128)S(1)} %get-tuple-element.25.own_ref, f32[136,512]{1,0:T(8,128)S(1)} %collective-permute-done.3.other_ref), custom_call_target="tpu_custom_call" | custom-call | flops 67108864 | bytes 1048576 | tf_op jit(solution)/shard_map/pallas_call | solution.py:252
  (2 shorter events, 0.1 us)
Async XLA Ops:
  1.8 11.9 %collective-permute-start.4 = (bf16[128,512]{1,0:T(8,128)(2,1)S(1)}, bf16[128,512]{1,0:T(8,128)(2,1)S(1)}, u32[]{:S(2)}, u32[]{:S(2)}) collective-permute-start(bf16[128,512]{1,0:T(8,128)(2,1)S(1)} %get-tuple-element.27.refs_0_), channel_id=1, source_target_pairs={{0,2},{2,0},{4,6},{6,4},{8,10},{10,8},{12,14},{14,12},{1,3},{3,1},... | collective-permute-start | bytes 393224 | tf_op jit(solution)/shard_map/ppermute | solution.py:270
  2.4 7.8 %collective-permute-start.1 = (bf16[128,256]{1,0:T(8,128)(2,1)S(1)}, bf16[128,256]{1,0:T(8,128)(2,1)S(1)}, u32[]{:S(2)}, u32[]{:S(2)}) collective-permute-start(bf16[128,256]{1,0:T(8,128)(2,1)S(1)} %get-tuple-element.24.refs_0_), channel_id=1, source_target_pairs={{0,8},{2,10},{4,12},{6,14},{8,0},{10,2},{12,4},{14,6},{1,9},{3,11}... | collective-permute-start | bytes 196616 | tf_op jit(solution)/shard_map/ppermute | solution.py:270
  6.0 8.9 %collective-permute-start.5 = (bf16[128,512]{1,0:T(8,128)(2,1)S(1)}, bf16[128,512]{1,0:T(8,128)(2,1)S(1)}, u32[]{:S(2)}, u32[]{:S(2)}) collective-permute-start(bf16[128,512]{1,0:T(8,128)(2,1)S(1)} %get-tuple-element.28.refs_2_), channel_id=1, source_target_pairs={{0,2},{2,0},{4,6},{6,4},{8,10},{10,8},{12,14},{14,12},{1,3},{3,1},... | collective-permute-start | bytes 393224 | tf_op jit(solution)/shard_map/ppermute | solution.py:270
  6.2 6.7 %collective-permute-start.7 = (bf16[128,256]{1,0:T(8,128)(2,1)S(1)}, bf16[128,256]{1,0:T(8,128)(2,1)S(1)}, u32[]{:S(2)}, u32[]{:S(2)}) collective-permute-start(bf16[128,256]{1,0:T(8,128)(2,1)S(1)} %get-tuple-element.31.refs_0_), channel_id=1, source_target_pairs={{0,8},{2,10},{4,12},{6,14},{8,0},{10,2},{12,4},{14,6},{1,9},{3,11}... | collective-permute-start | bytes 196616 | tf_op jit(solution)/shard_map/ppermute | solution.py:270
  6.5 13.3 %collective-permute-start = (bf16[128,512]{1,0:T(8,128)(2,1)S(1)}, bf16[128,512]{1,0:T(8,128)(2,1)S(1)}, u32[]{:S(2)}, u32[]{:S(2)}) collective-permute-start(bf16[128,512]{1,0:T(8,128)(2,1)S(1)} %get-tuple-element.23.refs_0_), channel_id=1, source_target_pairs={{0,2},{2,0},{4,6},{6,4},{8,10},{10,8},{12,14},{14,12},{1,3},{3,1},... | collective-permute-start | bytes 393224 | tf_op jit(solution)/shard_map/ppermute | solution.py:270
  10.2 9.6 %collective-permute-start.2 = (bf16[256,256]{1,0:T(8,128)(2,1)S(1)}, bf16[256,256]{1,0:T(8,128)(2,1)S(1)}, u32[]{:S(2)}, u32[]{:S(2)}) collective-permute-start(bf16[256,256]{1,0:T(8,128)(2,1)S(1)} %shard_map.113.refs_0_), channel_id=1, source_target_pairs={{0,4},{2,6},{4,0},{6,2},{8,12},{10,14},{12,8},{14,10},{1,5},{3,7},... | collective-permute-start | bytes 393224 | tf_op jit(solution)/shard_map/ppermute | solution.py:270
  12.9 5.2 %collective-permute-start.6 = (bf16[128,256]{1,0:T(8,128)(2,1)S(1)}, bf16[128,256]{1,0:T(8,128)(2,1)S(1)}, u32[]{:S(2)}, u32[]{:S(2)}) collective-permute-start(bf16[128,256]{1,0:T(8,128)(2,1)S(1)} %get-tuple-element.31.refs_0_), channel_id=1, source_target_pairs={{0,4},{2,6},{4,0},{6,2},{8,12},{10,14},{12,8},{14,10},{1,5},{3,7},... | collective-permute-start | bytes 196616 | tf_op jit(solution)/shard_map/ppermute | solution.py:270
  13.7 5.2 %collective-permute-start.8 = (bf16[128,256]{1,0:T(8,128)(2,1)S(1)}, bf16[128,256]{1,0:T(8,128)(2,1)S(1)}, u32[]{:S(2)}, u32[]{:S(2)}) collective-permute-start(bf16[128,256]{1,0:T(8,128)(2,1)S(1)} %collective-permute-done.7.refs_2_), channel_id=1, source_target_pairs={{0,4},{2,6},{4,0},{6,2},{8,12},{10,14},{12,8},{14,10},{1,5},{3,7},... | collective-permute-start | bytes 196616 | tf_op jit(solution)/shard_map/ppermute | solution.py:270
  19.7 2.2 %collective-permute-start.9 = (f32[8,1024]{1,0:T(8,128)S(1)}, f32[8,1024]{1,0:T(8,128)S(1)}, u32[]{:S(2)}, u32[]{:S(2)}) collective-permute-start(f32[8,1024]{1,0:T(8,128)S(1)} %shard_map.117.mine_ref), channel_id=1, source_target_pairs={{0,2},{2,0},{4,6},{6,4},{8,10},{10,8},{12,14},{14,12},{1,3},{3,1},... | collective-permute-start | bytes 98312 | tf_op jit(solution)/shard_map/ppermute | solution.py:270
  21.3 14.5 %collective-permute-start.3 = (f32[136,512]{1,0:T(8,128)S(1)}, f32[136,512]{1,0:T(8,128)S(1)}, u32[]{:S(2)}, u32[]{:S(2)}) collective-permute-start(f32[136,512]{1,0:T(8,128)S(1)} %get-tuple-element.26), channel_id=1, source_target_pairs={{0,2},{2,0},{4,6},{6,4},{8,10},{10,8},{12,14},{14,12},{1,3},{3,1},... | collective-permute-start | bytes 835592 | tf_op jit(solution)/shard_map/ppermute | solution.py:270
  22.9 12.0 %collective-permute-start.10 = (f32[128,512]{1,0:T(8,128)S(1)}, f32[128,512]{1,0:T(8,128)S(1)}, u32[]{:S(2)}, u32[]{:S(2)}) collective-permute-start(f32[128,512]{1,0:T(8,128)S(1)} %get-tuple-element.33), channel_id=1, source_target_pairs={{0,2},{2,0},{4,6},{6,4},{8,10},{10,8},{12,14},{14,12},{1,3},{3,1},... | collective-permute-start | bytes 786440 | tf_op jit(solution)/shard_map/ppermute | solution.py:270
  23.0 5.2 %collective-permute-start.11 = (bf16[128,256]{1,0:T(8,128)(2,1)S(1)}, bf16[128,256]{1,0:T(8,128)(2,1)S(1)}, u32[]{:S(2)}, u32[]{:S(2)}) collective-permute-start(bf16[128,256]{1,0:T(8,128)(2,1)S(1)} %get-tuple-element.35), channel_id=1, source_target_pairs={{0,4},{2,6},{4,0},{6,2},{8,12},{10,14},{12,8},{14,10},{1,5},{3,7},... | collective-permute-start | bytes 196616 | tf_op jit(solution)/shard_map/ppermute | solution.py:270
  24.8 7.7 %collective-permute-start.12 = (bf16[128,256]{1,0:T(8,128)(2,1)S(1)}, bf16[128,256]{1,0:T(8,128)(2,1)S(1)}, u32[]{:S(2)}, u32[]{:S(2)}) collective-permute-start(bf16[128,256]{1,0:T(8,128)(2,1)S(1)} %get-tuple-element.36), channel_id=1, source_target_pairs={{0,8},{2,10},{4,12},{6,14},{8,0},{10,2},{12,4},{14,6},{1,9},{3,11}... | collective-permute-start | bytes 196616 | tf_op jit(solution)/shard_map/ppermute | solution.py:270
  28.2 6.1 %collective-permute-start.13 = (bf16[128,256]{1,0:T(8,128)(2,1)S(1)}, bf16[128,256]{1,0:T(8,128)(2,1)S(1)}, u32[]{:S(2)}, u32[]{:S(2)}) collective-permute-start(bf16[128,256]{1,0:T(8,128)(2,1)S(1)} %get-tuple-element.37), channel_id=1, source_target_pairs={{0,12},{2,14},{4,8},{6,10},{8,4},{10,6},{12,0},{14,2},{1,13},{3,15... | collective-permute-start | bytes 196616 | tf_op jit(solution)/shard_map/ppermute | solution.py:270
where the time goes:
time: 36.8 us; the launch traced here: 36.7 us
  starting transfers between devices  14.8 us (40%)
  waiting for transfers between devices  14.1 us (38%)
  Pallas kernels  7.06 us (19%)
  between operations  0.71 us (2%)
    ppermute x14, starting transfers between devices, swapped(): return lax.ppermute(x, 'context', [(i, i ^ bits) for i in range(devices)])  14.8 us
    ppermute x14, waiting for transfers between devices, swapped(): return lax.ppermute(x, 'context', [(i, i ^ bits) for i in range(devices)])  14.1 us
    pallas_call x10, Pallas kernels, call(): pl.pallas_call(kernel, out_shape=outs, in_specs=specs, out_specs=jax.tree...  7.06 us
  transfers between devices with their start and end apart: 14, of which 6 were waited for; matrix products, arithmetic and copies ran while one was open for 0% of the time, Pallas kernels for 14%

commit v1 on v0

--- a/solution.py
+++ b/solution.py
@@ -64,13 +64,18 @@
     return jnp.concatenate(parts, axis=0)
 
 
-def fetch_kernel(s, owner, ka, va, qa, ga, kb, vb, qb, kv_a, kv_b, query_a, grad_a, query_b, gap, slabs, sems):
-    cols = [pl.ds(i * s.dim, s.dim) for i in range(2)]
-    moves = [
-        (owner, slabs), (ka, kv_a.at[:, cols[0]]), (va, kv_a.at[:, cols[1]]),
-        (kb, kv_b.at[:, cols[0]]), (vb, kv_b.at[:, cols[1]]),
-        (qa, query_a), (ga, grad_a), (qb, query_b),
-    ]
+def fetch_kernel(s, keys, values, out, sems):
+    left = pltpu.make_async_copy(keys, out.at[:, pl.ds(0, s.dim)], sems.at[0])
+    right = pltpu.make_async_copy(values, out.at[:, pl.ds(s.dim, s.dim)], sems.at[1])
+    left.start()
+    right.start()
+    left.wait()
+    right.wait()
+
+
+def fetch_rest_kernel(s, owner, kb, vb, qa, ga, qb, kv_b, rows, gap, slabs, sems):
+    moves = [(owner, slabs), (kb, kv_b.at[:, pl.ds(0, s.dim)]), (vb, kv_b.at[:, pl.ds(s.dim, s.dim)])]
+    moves += [(x, rows.at[:, pl.ds(i * s.width, s.width)]) for i, x in enumerate((qa, ga, qb))]
     copies = [pltpu.make_async_copy(a, b, sems.at[i]) for i, (a, b) in enumerate(moves)]
     for c in copies:
         c.start()
@@ -84,17 +89,10 @@
         c.wait()
 
 
-def stack_kernel(s, *refs):
-    count = len(refs) // 3
-    for i in range(count):
-        refs[2 * count + i][...] = stacked(s, refs[2 * i], refs[2 * i + 1])
-
-
-def pack_kernel(*refs):
-    at = 0
-    for ref in refs[:-1]:
-        refs[-1][at:at + ref.shape[0]] = ref[...]
-        at += ref.shape[0]
+def stack_kernel(s, own_ref, other_ref, *out_refs):
+    for i, ref in enumerate(out_refs):
+        cols = slice(i * s.width, (i + 1) * s.width)
+        ref[...] = stacked(s, own_ref[:, cols], other_ref[:, cols])
 
 
 def stats_kernel(s, gap_ref, q_ref, g_ref, *refs):
@@ -179,39 +177,43 @@
         ref[:, group:] = high_rows[:, d * group:(d + 1) * group]
 
 
-def forward_kernel(s, names, gap_ref, q_ref, *refs):
-    chunks, outs = refs[:-2], refs[-2:]
-    q = q_ref[...]
-    blocks = [r[k * s.tok:(k + 1) * s.tok] for r in chunks for k in range(r.shape[0] // s.tok)]
-    blocks = [blocks[names.index(k)] for k in range(s.chunks)]
-    k_low, k_high = halves(s, blocks, 0)
-    v_low, v_high = halves(s, blocks, 1)
+def forward_rows(s, d, gap_ref, q_ref, chunks, out_ref):
+    k_low, k_high = halves(s, chunks, 0)
+    v_low, v_high = halves(s, chunks, 1)
     rel = relative(s)
     for h in range(2):
-        for d in range(2):
-            at = (2 * h + d) * s.group
-            qt = q[at:at + s.group]
-            raw = dot(k_low, qt, ((1,), (1,)))
-            if h == 0:
-                blocks = [(masked(s, raw, rel, gap_ref, d, False), v_low)]
-            else:
-                more = dot(k_high, qt, ((1,), (1,)))
-                more = masked(s, more, rel, gap_ref, d, True)
-                blocks = [(raw, v_low), (more, v_high)]
-            top = jnp.full((1, s.group), FLOOR, F32)
-            for raw, vv in blocks:
-                top = jnp.maximum(top, jnp.max(raw, axis=0, keepdims=True))
-            total = jnp.zeros((1, s.group), F32)
-            acc = jnp.zeros((s.dim, s.group), F32)
-            for raw, vv in blocks:
-                p = jnp.exp2((raw - top) * s.exp_scale)
-                total = total + jnp.sum(p, axis=0, keepdims=True)
-                acc = acc + dot(vv, p.astype(BF16), ((0,), (0,)))
-            cols = slice(h * s.group, (h + 1) * s.group)
-            outs[d][:s.dim, cols] = acc
-            outs[d][s.dim:s.dim + 1, cols] = top
-            outs[d][s.dim + 1:s.dim + 2, cols] = total
-            outs[d][s.dim + 2:s.dim + 8, cols] = jnp.zeros((6, s.group), F32)
+        at = (2 * h + d) * s.group
+        qt = q_ref[at:at + s.group]
+        raw = dot(k_low, qt, ((1,), (1,)))
+        if h == 0:
+            blocks = [(masked(s, raw, rel, gap_ref, d, False), v_low)]
+        else:
+            more = dot(k_high, qt, ((1,), (1,)))
+            blocks = [(raw, v_low), (masked(s, more, rel, gap_ref, d, True), v_high)]
+        top = jnp.full((1, s.group), FLOOR, F32)
+        for raw, vv in blocks:
+            top = jnp.maximum(top, jnp.max(raw, axis=0, keepdims=True))
+        total = jnp.zeros((1, s.group), F32)
+        acc = jnp.zeros((s.dim, s.group), F32)
+        for raw, vv in blocks:
+            p = jnp.exp2((raw - top) * s.exp_scale)
+            total = total + jnp.sum(p, axis=0, keepdims=True)
+            acc = acc + dot(vv, p.astype(BF16), ((0,), (0,)))
+        cols = slice(h * s.group, (h + 1) * s.group)
+        out_ref[:s.dim, cols] = acc
+        out_ref[s.dim:s.dim + 1, cols] = top
+        out_ref[s.dim + 1:s.dim + 2, cols] = total
+        out_ref[s.dim + 2:s.dim + 8, cols] = jnp.zeros((6, s.group), F32)
+
+
+def other_kernel(s, gap_ref, q_ref, dq_ref, *refs):
+    chunks, out_ref = refs[:-1], refs[-1]
+    forward_rows(s, 1, gap_ref, q_ref, chunks, out_ref)
+    out_ref[s.dim + 8:, :] = dq_ref[...]
+
+
+def own_kernel(s, gap_ref, q_ref, after, *refs):
+    forward_rows(s, 0, gap_ref, q_ref, refs[:-1], refs[-1])
 
 
 def rows_from(s, wide, out_ref):
@@ -222,18 +224,15 @@
             out_ref[h * s.half:(h + 1) * s.half, g * s.dim:(g + 1) * s.dim] = block.T.astype(BF16)
 
 
-def query_kernel(s, own_ref, other_ref, out_ref):
-    rows_from(s, (own_ref[...] + other_ref[...]) * s.scale, out_ref)
-
-
-def merge_kernel(s, own_ref, other_ref, out_ref):
+def rows_kernel(s, own_ref, dq_ref, got_ref, out_ref, query_ref):
     d = s.dim
+    rows_from(s, (dq_ref[...] + got_ref[d + 8:, :]) * s.scale, query_ref)
     m1, l1 = own_ref[d:d + 1, :], own_ref[d + 1:d + 2, :]
-    m2, l2 = other_ref[d:d + 1, :], other_ref[d + 1:d + 2, :]
+    m2, l2 = got_ref[d:d + 1, :], got_ref[d + 1:d + 2, :]
     top = jnp.maximum(m1, m2)
     w1, w2 = jnp.exp2((m1 - top) * s.exp_scale), jnp.exp2((m2 - top) * s.exp_scale)
     total = l1 * w1 + l2 * w2
-    rows_from(s, own_ref[:d, :] * (w1 / total) + other_ref[:d, :] * (w2 / total), out_ref)
+    rows_from(s, own_ref[:d, :] * (w1 / total) + got_ref[:d, :] * (w2 / total), out_ref)
 
 
 def sum_kernel(s, *refs):
@@ -273,29 +272,23 @@
         return jax.ShapeDtypeStruct(shape, dtype)
 
     unit = 2 * 4 * group * s.keys * dim
-    wide, pair, stack = sds((tok, width), BF16), sds((tok, 2 * dim), BF16), sds((4 * group, dim), BF16)
-    kv_a, kv_b, query_a, grad_a, query_b, gap = call(
-        partial(fetch_kernel, s), [pair, pair, wide, wide, wide, sds((2 * s.chunks, group), jnp.int32)],
-        [slab_owner, key_a, value_a, query_a, grad_out_a, key_b, value_b, query_b], unit,
-        space=pltpu.HBM, scratch=[pltpu.SMEM((devices,), jnp.int32), pltpu.SemaphoreType.DMA((8,))],
-    )
-    held, bit = {0: kv_a}, s.chunks // 2
-    while bit:
-        held.update({k ^ bit: swapped(x, 2 * bit) for k, x in list(held.items())})
-        bit //= 2
-    kv_a = [held[k] for k in range(s.chunks)]
-    query_p, grad_p = swapped(query_a, 1), swapped(grad_a, 1)
-    query_bp = swapped(query_b, 1)
-    q_a, g_a = call(partial(stack_kernel, s), [stack, stack], [query_a, query_p, grad_a, grad_p], unit)
+    pair, stack = sds((tok, 2 * dim), BF16), sds((4 * group, dim), BF16)
+    kv_a = call(
+        partial(fetch_kernel, s), pair, [key_a, value_a], unit,
+        space=pltpu.HBM, scratch=[pltpu.SemaphoreType.DMA((2,))],
+    )
+    near = [swapped(kv_a, 2 * k) for k in range(1, s.chunks)]
+    kv_b, rows, gap = call(
+        partial(fetch_rest_kernel, s),
+        [pair, sds((tok, 3 * width), BF16), sds((2 * s.chunks, group), jnp.int32)],
+        [slab_owner, key_b, value_b, query_a, grad_out_a, query_b], unit,
+        space=pltpu.HBM, scratch=[pltpu.SMEM((devices,), jnp.int32), pltpu.SemaphoreType.DMA((6,))],
+    )
+    kv_a = [kv_a] + near
+    rows_p = swapped(rows, 1)
+    kv_b = [kv_b] + [swapped(kv_b, 2 * k) for k in range(1, s.chunks)]
+    q_a, g_a, q_b = call(partial(stack_kernel, s), [stack] * 3, [rows, rows_p], unit)
     mine = call(partial(stats_kernel, s), sds((8, 4 * group), F32), [gap, q_a, g_a, *kv_a], 8 * unit)
-    order_b, bit = [0], s.chunks // 2
-    while bit:
-        if len(order_b) > 1:
-            kv_b = call(pack_kernel, sds((len(order_b) * tok, 2 * dim), BF16), parts, unit)
-        parts = [kv_b, swapped(kv_b, 2 * bit)]
-        order_b += [k ^ bit for k in order_b]
-        bit //= 2
-    kv_b = parts
     theirs = swapped(mine, 1)
     kinds = [F32] + [BF16] * (s.chunks - 1)
     back = call(
@@ -306,16 +299,13 @@
     )
     terms, (dq_own, dq_other) = back[:s.chunks], back[s.chunks:]
     terms = [terms[0]] + [swapped(terms[k], 2 * k) for k in range(1, s.chunks)]
-    dq_got = swapped(dq_other, 1)
-
-    (q_b,) = call(partial(stack_kernel, s), [stack], [query_b, query_bp], unit)
-    part_own, part_other = call(
-        partial(forward_kernel, s, order_b), [sds((dim + 8, 2 * group), F32)] * 2,
-        [gap, q_b, *kv_b], 10 * unit,
-    )
-    part_got = swapped(part_other, 1)
-    grad_query_a = call(partial(query_kernel, s), sds((tok, width), BF16), [dq_own, dq_got], unit)
-    out_b = call(partial(merge_kernel, s), sds((tok, width), BF16), [part_own, part_got], unit)
+    send = call(
+        partial(other_kernel, s), sds((2 * dim + 8, 2 * group), F32),
+        [gap, q_b, dq_other, *kv_b], 5 * unit,
+    )
+    got = swapped(send, 1)
+    part = call(partial(own_kernel, s), sds((dim + 8, 2 * group), F32), [gap, q_b, send, *kv_b], 5 * unit)
+    out_b, grad_query_a = call(partial(rows_kernel, s), [sds((tok, width), BF16)] * 2, [part, dq_own, got], unit)
     grad_key_a, grad_value_a = call(partial(sum_kernel, s), [sds((tok, dim), BF16)] * 2, terms, unit)
     return (out_b, grad_query_a, grad_key_a, grad_value_a)
 

time: 36.8 us -> 37.6 us (1.022)
  waiting for transfers between devices: 14.1 us -> 14.8 us
    ppermute x14 -> x12, waiting for transfers between devices: 14.1 us -> 14.8 us  [swapped(): return lax.ppermute(x, 'context', [(i, i ^ bits) for i in range(devices)])]
    ppermute x14 -> x12, starting transfers between devices: 14.8 us -> 14.8 us  [swapped(): return lax.ppermute(x, 'context', [(i, i ^ bits) for i in range(devices)])]
    pallas_call x10 -> x9, Pallas kernels: 7.06 us -> 7.09 us  [call(): pl.pallas_call(kernel, out_shape=outs, in_specs=specs, out_specs=jax.tree...]
  transfers between devices with their start and end apart: 14 -> 12, of which waited for: 6 -> 4; matrix products, arithmetic and copies ran while one was open for 0% -> 0% of each run, Pallas kernels for 14% -> 9%
where the time goes in v1:
time: 37.6 us; the launch traced here: 37.4 us
  starting transfers between devices  14.8 us (39%)
  waiting for transfers between devices  14.8 us (39%)
  Pallas kernels  7.09 us (19%)
  between operations  0.71 us (2%)
    ppermute x12, starting transfers between devices, swapped(): return lax.ppermute(x, 'context', [(i, i ^ bits) for i in range(devices)])  14.8 us
    ppermute x12, waiting for transfers between devices, swapped(): return lax.ppermute(x, 'context', [(i, i ^ bits) for i in range(devices)])  14.8 us
    pallas_call x9, Pallas kernels, call(): pl.pallas_call(kernel, out_shape=outs, in_specs=specs, out_specs=jax.tree...  7.09 us
  transfers between devices with their start and end apart: 12, of which 4 were waited for; matrix products, arithmetic and copies ran while one was open for 0% of the time, Pallas kernels for 9%

profile of v1, /device:TPU:0, one launch (start us, length us, event | category | flops | bytes accessed | tf_op | source)
XLA Modules:
  0.0 37.4 jit_solution(18030197981987651072)
XLA Ops:
  0.6 1.1 %shard_map.111 = (bf16[128,256]{1,0:T(8,128)(2,1)S(1)}, bf16[128,1536]{1,0:T(8,128)(2,1)S(1)}, s32[8,256]{1,0:T(8,128)S(1)}) custom-call(s32[8]{0:T(128)} %owner.1, bf16[128,128]{1,0:T(8,128)(2,1)} %kb.1, bf16[128,128]{1,0:T(8,128)(2,1)} %vb.1, bf16[128,512]{1,0:T(8,128)(2,1)} %qa.1, bf16[128,512]{1,0:T(8,128)(2,1)} %ga.1, bf16[128,512]{1,0:T(8,128)(2,1)} %qb.1), custom_call_target="tpu_custom_call" | custom-call | flops 67108864 | bytes 1048576 | tf_op jit(solution)/shard_map/pallas_call | solution.py:251
  1.8 0.6 %collective-permute-start = (bf16[128,1536]{1,0:T(8,128)(2,1)S(1)}, bf16[128,1536]{1,0:T(8,128)(2,1)S(1)}, u32[]{:S(2)}, u32[]{:S(2)}) collective-permute-start(bf16[128,1536]{1,0:T(8,128)(2,1)S(1)} %get-tuple-element.21.own_ref), channel_id=1, source_target_pairs={{0,2},{2,0},{4,6},{6,4},{8,10},{10,8},{12,14},{14,12},{1,3},{3,1},... | collective-permute-start | bytes 1179656 | tf_op jit(solution)/shard_map/ppermute | solution.py:269
  2.3 0.8 %shard_map.113.refs_0_ = bf16[128,256]{1,0:T(8,128)(2,1)S(1)} custom-call(bf16[128,128]{1,0:T(8,128)(2,1)} %keys.1, bf16[128,128]{1,0:T(8,128)(2,1)} %values.1), custom_call_target="tpu_custom_call" | custom-call | flops 67108864 | bytes 1048576 | tf_op jit(solution)/shard_map/pallas_call | solution.py:251
  3.1 2.6 %collective-permute-start.1 = (bf16[128,256]{1,0:T(8,128)(2,1)S(1)}, bf16[128,256]{1,0:T(8,128)(2,1)S(1)}, u32[]{:S(2)}, u32[]{:S(2)}) collective-permute-start(bf16[128,256]{1,0:T(8,128)(2,1)S(1)} %shard_map.113.refs_0_), channel_id=1, source_target_pairs={{0,4},{2,6},{4,0},{6,2},{8,12},{10,14},{12,8},{14,10},{1,5},{3,7},... | collective-permute-start | bytes 196616 | tf_op jit(solution)/shard_map/ppermute | solution.py:269
  5.8 2.6 %collective-permute-start.2 = (bf16[128,256]{1,0:T(8,128)(2,1)S(1)}, bf16[128,256]{1,0:T(8,128)(2,1)S(1)}, u32[]{:S(2)}, u32[]{:S(2)}) collective-permute-start(bf16[128,256]{1,0:T(8,128)(2,1)S(1)} %shard_map.113.refs_0_), channel_id=1, source_target_pairs={{0,8},{2,10},{4,12},{6,14},{8,0},{10,2},{12,4},{14,6},{1,9},{3,11}... | collective-permute-start | bytes 196616 | tf_op jit(solution)/shard_map/ppermute | solution.py:269
  8.4 0.0 collective-permute-start.3
  8.4 0.0 collective-permute-done.other_ref
  8.4 0.1 shard_map.112
  8.5 0.0 collective-permute-done.1.refs_1_
  8.5 4.3 %collective-permute-done.2.refs_2_ = bf16[128,256]{1,0:T(8,128)(2,1)S(1)} collective-permute-done((bf16[128,256]{1,0:T(8,128)(2,1)S(1)}, bf16[128,256]{1,0:T(8,128)(2,1)S(1)}, u32[]{:S(2)}, u32[]{:S(2)}) %collective-permute-start.2) | collective-permute-done | bytes 65568 | tf_op jit(solution)/shard_map/ppermute | solution.py:269
  12.8 1.6 %collective-permute-done.3.refs_3_ = bf16[128,256]{1,0:T(8,128)(2,1)S(1)} collective-permute-done((bf16[128,256]{1,0:T(8,128)(2,1)S(1)}, bf16[128,256]{1,0:T(8,128)(2,1)S(1)}, u32[]{:S(2)}, u32[]{:S(2)}) %collective-permute-start.3) | collective-permute-done | bytes 65568 | tf_op jit(solution)/shard_map/ppermute | solution.py:269
  14.4 0.8 %shard_map.114.mine_ref = f32[8,1024]{1,0:T(8,128)S(1)} custom-call(s32[8,256]{1,0:T(8,128)S(1)} %get-tuple-element.20.gap_ref, bf16[1024,128]{1,0:T(8,128)(2,1)S(1)} %get-tuple-element.23.q_ref, bf16[1024,128]{1,0:T(8,128)(2,1)S(1)} %get-tuple-element.24.g_ref, bf16[128,256]{1,0:T(8,128)(2,1)S(1)} %shard_map.113.refs_0_, ...), custom_call_target="tpu_custom_call" | custom-call | flops 536870912 | bytes 1048576 | tf_op jit(solution)/shard_map/pallas_call | solution.py:251
  15.2 0.1 collective-permute-start.4
  15.3 1.3 %collective-permute-start.5 = (bf16[128,256]{1,0:T(8,128)(2,1)S(1)}, bf16[128,256]{1,0:T(8,128)(2,1)S(1)}, u32[]{:S(2)}, u32[]{:S(2)}) collective-permute-start(bf16[128,256]{1,0:T(8,128)(2,1)S(1)} %get-tuple-element.26.refs_0_), channel_id=1, source_target_pairs={{0,4},{2,6},{4,0},{6,2},{8,12},{10,14},{12,8},{14,10},{1,5},{3,7},... | collective-permute-start | bytes 196616 | tf_op jit(solution)/shard_map/ppermute | solution.py:269
  16.6 1.7 %collective-permute-start.6 = (bf16[128,256]{1,0:T(8,128)(2,1)S(1)}, bf16[128,256]{1,0:T(8,128)(2,1)S(1)}, u32[]{:S(2)}, u32[]{:S(2)}) collective-permute-start(bf16[128,256]{1,0:T(8,128)(2,1)S(1)} %get-tuple-element.26.refs_0_), channel_id=1, source_target_pairs={{0,8},{2,10},{4,12},{6,14},{8,0},{10,2},{12,4},{14,6},{1,9},{3,11}... | collective-permute-start | bytes 196616 | tf_op jit(solution)/shard_map/ppermute | solution.py:269
  18.4 1.4 %collective-permute-start.7 = (bf16[128,256]{1,0:T(8,128)(2,1)S(1)}, bf16[128,256]{1,0:T(8,128)(2,1)S(1)}, u32[]{:S(2)}, u32[]{:S(2)}) collective-permute-start(bf16[128,256]{1,0:T(8,128)(2,1)S(1)} %get-tuple-element.26.refs_0_), channel_id=1, source_target_pairs={{0,12},{2,14},{4,8},{6,10},{8,4},{10,6},{12,0},{14,2},{1,13},{3,15... | collective-permute-start | bytes 196616 | tf_op jit(solution)/shard_map/ppermute | solution.py:269
  19.7 0.0 collective-permute-done.4.theirs_ref
  19.7 1.1 %shard_map.115 = (f32[128,256]{1,0:T(8,128)S(1)}, bf16[128,256]{1,0:T(8,128)(2,1)S(1)}, bf16[128,256]{1,0:T(8,128)(2,1)S(1)}, bf16[128,256]{1,0:T(8,128)(2,1)S(1...) custom-call(s32[8,256]{1,0:T(8,128)S(1)} %get-tuple-element.20.gap_ref, ...), custom_call_target="tpu_custom_call" | custom-call | flops 1342177280 | bytes 1048576 | tf_op jit(solution)/shard_map/pallas_call | solution.py:251
  20.8 0.0 collective-permute-done.5.refs_1_
  20.8 4.2 %collective-permute-done.6.refs_2_ = bf16[128,256]{1,0:T(8,128)(2,1)S(1)} collective-permute-done((bf16[128,256]{1,0:T(8,128)(2,1)S(1)}, bf16[128,256]{1,0:T(8,128)(2,1)S(1)}, u32[]{:S(2)}, u32[]{:S(2)}) %collective-permute-start.6) | collective-permute-done | bytes 65568 | tf_op jit(solution)/shard_map/ppermute | solution.py:269
  25.0 0.0 collective-permute-done.7.refs_3_
  25.0 0.8 %shard_map.116.after = f32[264,512]{1,0:T(8,128)S(1)} custom-call(s32[8,256]{1,0:T(8,128)S(1)} %get-tuple-element.20.gap_ref, bf16[1024,128]{1,0:T(8,128)(2,1)S(1)} %get-tuple-element.22.q_ref, f32[128,512]{1,0:T(8,128)S(1)} %get-tuple-element.25.dq_ref, bf16[128,256]{1,0:T(8,128)(2,1)S(1)} %get-tuple-element.26.refs_0_, ...), custom_call_target="tpu_custom_call" | custom-call | flops 335544320 | bytes 1048576 | tf_op jit(solution)/shard_map/pallas_call | solution.py:251
  25.8 0.1 collective-permute-start.8
  25.9 1.5 %collective-permute-start.9 = (bf16[128,256]{1,0:T(8,128)(2,1)S(1)}, bf16[128,256]{1,0:T(8,128)(2,1)S(1)}, u32[]{:S(2)}, u32[]{:S(2)}) collective-permute-start(bf16[128,256]{1,0:T(8,128)(2,1)S(1)} %get-tuple-element.31), channel_id=1, source_target_pairs={{0,4},{2,6},{4,0},{6,2},{8,12},{10,14},{12,8},{14,10},{1,5},{3,7},... | collective-permute-start | bytes 196616 | tf_op jit(solution)/shard_map/ppermute | solution.py:269
  27.4 1.3 %collective-permute-start.10 = (bf16[128,256]{1,0:T(8,128)(2,1)S(1)}, bf16[128,256]{1,0:T(8,128)(2,1)S(1)}, u32[]{:S(2)}, u32[]{:S(2)}) collective-permute-start(bf16[128,256]{1,0:T(8,128)(2,1)S(1)} %get-tuple-element.32), channel_id=1, source_target_pairs={{0,8},{2,10},{4,12},{6,14},{8,0},{10,2},{12,4},{14,6},{1,9},{3,11}... | collective-permute-start | bytes 196616 | tf_op jit(solution)/shard_map/ppermute | solution.py:269
  28.7 1.6 %collective-permute-start.11 = (bf16[128,256]{1,0:T(8,128)(2,1)S(1)}, bf16[128,256]{1,0:T(8,128)(2,1)S(1)}, u32[]{:S(2)}, u32[]{:S(2)}) collective-permute-start(bf16[128,256]{1,0:T(8,128)(2,1)S(1)} %get-tuple-element.33), channel_id=1, source_target_pairs={{0,12},{2,14},{4,8},{6,10},{8,4},{10,6},{12,0},{14,2},{1,13},{3,15... | collective-permute-start | bytes 196616 | tf_op jit(solution)/shard_map/ppermute | solution.py:269
  30.3 0.8 %shard_map.117.own_ref = f32[136,512]{1,0:T(8,128)S(1)} custom-call(s32[8,256]{1,0:T(8,128)S(1)} %get-tuple-element.20.gap_ref, bf16[1024,128]{1,0:T(8,128)(2,1)S(1)} %get-tuple-element.22.q_ref, f32[264,512]{1,0:T(8,128)S(1)} %shard_map.116.after, bf16[128,256]{1,0:T(8,128)(2,1)S(1)} %get-tuple-element.26.refs_0_, ...), custom_call_target="tpu_custom_call" | custom-call | flops 335544320 | bytes 1048576 | tf_op jit(solution)/shard_map/pallas_call | solution.py:251
  31.1 0.0 collective-permute-done.9.refs_1_
  31.1 4.7 %collective-permute-done.10.refs_2_ = bf16[128,256]{1,0:T(8,128)(2,1)S(1)} collective-permute-done((bf16[128,256]{1,0:T(8,128)(2,1)S(1)}, bf16[128,256]{1,0:T(8,128)(2,1)S(1)}, u32[]{:S(2)}, u32[]{:S(2)}) %collective-permute-start.10) | collective-permute-done | bytes 65568 | tf_op jit(solution)/shard_map/ppermute | solution.py:269
  35.8 0.0 collective-permute-done.11.refs_3_
  35.8 0.7 %shard_map.119 = (bf16[128,128]{1,0:T(8,128)(2,1)}, bf16[128,128]{1,0:T(8,128)(2,1)}) custom-call(f32[128,256]{1,0:T(8,128)S(1)} %get-tuple-element.30.refs_0_, bf16[128,256]{1,0:T(8,128)(2,1)S(1)} %collective-permute-done.9.refs_1_, bf16[128,256]{1,0:T(8,128)(2,1)S(1)} %collective-permute-done.10.refs_2_, bf16[128,256]{1,0:T(8,128)(2,1)S(1)} %collective-permute-done.11.refs_3_), custom_call_target="tpu_custom_call" | custom-call | flops 67108864 | bytes 1048576 | tf_op jit(solution)/shard_map/pallas_call | solution.py:251
  36.4 0.0 collective-permute-done.8.got_ref
  36.4 1.0 %shard_map.118 = (bf16[128,512]{1,0:T(8,128)(2,1)}, bf16[128,512]{1,0:T(8,128)(2,1)}) custom-call(f32[136,512]{1,0:T(8,128)S(1)} %shard_map.117.own_ref, f32[128,512]{1,0:T(8,128)S(1)} %get-tuple-element.27.dq_ref, f32[264,512]{1,0:T(8,128)S(1)} %collective-permute-done.8.got_ref), custom_call_target="tpu_custom_call" | custom-call | flops 67108864 | bytes 1048576 | tf_op jit(solution)/shard_map/pallas_call | solution.py:251
Async XLA Ops:
  1.8 6.6 %collective-permute-start = (bf16[128,1536]{1,0:T(8,128)(2,1)S(1)}, bf16[128,1536]{1,0:T(8,128)(2,1)S(1)}, u32[]{:S(2)}, u32[]{:S(2)}) collective-permute-start(bf16[128,1536]{1,0:T(8,128)(2,1)S(1)} %get-tuple-element.21.own_ref), channel_id=1, source_target_pairs={{0,2},{2,0},{4,6},{6,4},{8,10},{10,8},{12,14},{14,12},{1,3},{3,1},... | collective-permute-start | bytes 1179656 | tf_op jit(solution)/shard_map/ppermute | solution.py:269
  3.1 5.4 %collective-permute-start.1 = (bf16[128,256]{1,0:T(8,128)(2,1)S(1)}, bf16[128,256]{1,0:T(8,128)(2,1)S(1)}, u32[]{:S(2)}, u32[]{:S(2)}) collective-permute-start(bf16[128,256]{1,0:T(8,128)(2,1)S(1)} %shard_map.113.refs_0_), channel_id=1, source_target_pairs={{0,4},{2,6},{4,0},{6,2},{8,12},{10,14},{12,8},{14,10},{1,5},{3,7},... | collective-permute-start | bytes 196616 | tf_op jit(solution)/shard_map/ppermute | solution.py:269
  5.8 7.0 %collective-permute-start.2 = (bf16[128,256]{1,0:T(8,128)(2,1)S(1)}, bf16[128,256]{1,0:T(8,128)(2,1)S(1)}, u32[]{:S(2)}, u32[]{:S(2)}) collective-permute-start(bf16[128,256]{1,0:T(8,128)(2,1)S(1)} %shard_map.113.refs_0_), channel_id=1, source_target_pairs={{0,8},{2,10},{4,12},{6,14},{8,0},{10,2},{12,4},{14,6},{1,9},{3,11}... | collective-permute-start | bytes 196616 | tf_op jit(solution)/shard_map/ppermute | solution.py:269
  8.4 6.1 %collective-permute-start.3 = (bf16[128,256]{1,0:T(8,128)(2,1)S(1)}, bf16[128,256]{1,0:T(8,128)(2,1)S(1)}, u32[]{:S(2)}, u32[]{:S(2)}) collective-permute-start(bf16[128,256]{1,0:T(8,128)(2,1)S(1)} %shard_map.113.refs_0_), channel_id=1, source_target_pairs={{0,12},{2,14},{4,8},{6,10},{8,4},{10,6},{12,0},{14,2},{1,13},{3,15... | collective-permute-start | bytes 196616 | tf_op jit(solution)/shard_map/ppermute | solution.py:269
  15.2 4.5 %collective-permute-start.4 = (f32[8,1024]{1,0:T(8,128)S(1)}, f32[8,1024]{1,0:T(8,128)S(1)}, u32[]{:S(2)}, u32[]{:S(2)}) collective-permute-start(f32[8,1024]{1,0:T(8,128)S(1)} %shard_map.114.mine_ref), channel_id=1, source_target_pairs={{0,2},{2,0},{4,6},{6,4},{8,10},{10,8},{12,14},{14,12},{1,3},{3,1},... | collective-permute-start | bytes 98312 | tf_op jit(solution)/shard_map/ppermute | solution.py:269
  15.3 5.6 %collective-permute-start.5 = (bf16[128,256]{1,0:T(8,128)(2,1)S(1)}, bf16[128,256]{1,0:T(8,128)(2,1)S(1)}, u32[]{:S(2)}, u32[]{:S(2)}) collective-permute-start(bf16[128,256]{1,0:T(8,128)(2,1)S(1)} %get-tuple-element.26.refs_0_), channel_id=1, source_target_pairs={{0,4},{2,6},{4,0},{6,2},{8,12},{10,14},{12,8},{14,10},{1,5},{3,7},... | collective-permute-start | bytes 196616 | tf_op jit(solution)/shard_map/ppermute | solution.py:269
  16.6 8.4 %collective-permute-start.6 = (bf16[128,256]{1,0:T(8,128)(2,1)S(1)}, bf16[128,256]{1,0:T(8,128)(2,1)S(1)}, u32[]{:S(2)}, u32[]{:S(2)}) collective-permute-start(bf16[128,256]{1,0:T(8,128)(2,1)S(1)} %get-tuple-element.26.refs_0_), channel_id=1, source_target_pairs={{0,8},{2,10},{4,12},{6,14},{8,0},{10,2},{12,4},{14,6},{1,9},{3,11}... | collective-permute-start | bytes 196616 | tf_op jit(solution)/shard_map/ppermute | solution.py:269
  18.4 6.7 %collective-permute-start.7 = (bf16[128,256]{1,0:T(8,128)(2,1)S(1)}, bf16[128,256]{1,0:T(8,128)(2,1)S(1)}, u32[]{:S(2)}, u32[]{:S(2)}) collective-permute-start(bf16[128,256]{1,0:T(8,128)(2,1)S(1)} %get-tuple-element.26.refs_0_), channel_id=1, source_target_pairs={{0,12},{2,14},{4,8},{6,10},{8,4},{10,6},{12,0},{14,2},{1,13},{3,15... | collective-permute-start | bytes 196616 | tf_op jit(solution)/shard_map/ppermute | solution.py:269
  25.8 10.6 %collective-permute-start.8 = (f32[264,512]{1,0:T(8,128)S(1)}, f32[264,512]{1,0:T(8,128)S(1)}, u32[]{:S(2)}, u32[]{:S(2)}) collective-permute-start(f32[264,512]{1,0:T(8,128)S(1)} %shard_map.116.after), channel_id=1, source_target_pairs={{0,2},{2,0},{4,6},{6,4},{8,10},{10,8},{12,14},{14,12},{1,3},{3,1},... | collective-permute-start | bytes 1622024 | tf_op jit(solution)/shard_map/ppermute | solution.py:269
  25.9 5.2 %collective-permute-start.9 = (bf16[128,256]{1,0:T(8,128)(2,1)S(1)}, bf16[128,256]{1,0:T(8,128)(2,1)S(1)}, u32[]{:S(2)}, u32[]{:S(2)}) collective-permute-start(bf16[128,256]{1,0:T(8,128)(2,1)S(1)} %get-tuple-element.31), channel_id=1, source_target_pairs={{0,4},{2,6},{4,0},{6,2},{8,12},{10,14},{12,8},{14,10},{1,5},{3,7},... | collective-permute-start | bytes 196616 | tf_op jit(solution)/shard_map/ppermute | solution.py:269
  27.4 8.4 %collective-permute-start.10 = (bf16[128,256]{1,0:T(8,128)(2,1)S(1)}, bf16[128,256]{1,0:T(8,128)(2,1)S(1)}, u32[]{:S(2)}, u32[]{:S(2)}) collective-permute-start(bf16[128,256]{1,0:T(8,128)(2,1)S(1)} %get-tuple-element.32), channel_id=1, source_target_pairs={{0,8},{2,10},{4,12},{6,14},{8,0},{10,2},{12,4},{14,6},{1,9},{3,11}... | collective-permute-start | bytes 196616 | tf_op jit(solution)/shard_map/ppermute | solution.py:269
  28.7 7.1 %collective-permute-start.11 = (bf16[128,256]{1,0:T(8,128)(2,1)S(1)}, bf16[128,256]{1,0:T(8,128)(2,1)S(1)}, u32[]{:S(2)}, u32[]{:S(2)}) collective-permute-start(bf16[128,256]{1,0:T(8,128)(2,1)S(1)} %get-tuple-element.33), channel_id=1, source_target_pairs={{0,12},{2,14},{4,8},{6,10},{8,4},{10,6},{12,0},{14,2},{1,13},{3,15... | collective-permute-start | bytes 196616 | tf_op jit(solution)/shard_map/ppermute | solution.py:269
